TPU v7x, 32 devices: a whole 2x2x4 slice. The times are simulated.
32 devices in a mesh: cells: 8 (over z, y), coef: 4 (over x, core).
Axes of the slice: x: 2, y: 2, z: 4, core: 2. Of those that a mesh axis runs over, the one named last changes fastest.
Arguments:
- multipole: bfloat16 [128, 1024], P('coef', 'cells'), may hold values from -6 to 6
- parent_local: bfloat16 [128, 128], P('coef', 'cells'), may hold values from -6 to 6
- m2l_ops: bfloat16 [189, 128, 128], P(None, 'coef'), may hold values from -0.0390625 to 0.0390625
- l2l_ops: bfloat16 [8, 128, 128], P(None, 'coef'), may hold values from -0.5 to 0.5
- target_cell: int32 [189, 1024], P(None, 'cells'), may hold values from -1 to 1023, as said below
- particle_leaf: int32 [16384], P('cells'), may hold values from 0 to 1023, as said below
- particle_basis: bfloat16 [128, 16384], P('coef', 'cells'), may hold values from -0.5 to 0.5
Outputs:
- leaf_local: float32 [128, 1024], P('coef', 'cells')
- potential: float32 [16384], P('cells')
Inputs may be any that keep to these rules, and one draw needn't show every extreme that they name: `target_cell`: -1 marks an empty slot. Otherwise the target of source cell c lies on the device of c (cells are owned in blocks of 128: device c // 128) or on a device at most 2 indices away; from one device's source cells at most 256 pairs target the cells of any one other device, and some pair of devices has exactly 256. `particle_leaf`: the particles at positions d * 2048 to (d + 1) * 2048 - 1 lie in cells d * 128 to (d + 1) * 128 - 1.
All inputs are finite; a program needn't handle non-finite values.
Results may differ from a plain program's by a relative error of at most 0.0003.
Values may be sent and summed in bfloat16 or wider, within the bound.
A program may use at most 64 MiB of HBM per device.

v0:
```python
import functools

import jax
import jax.numpy as jnp
from jax import lax
from jax.experimental import pallas as pl
from jax.experimental.pallas import tpu as pltpu
from jax.sharding import PartitionSpec as P

REACH = 2
WINDOWS = tuple(w for r in range(REACH, 0, -1) for w in (-r, r))
GROUP = 16
NT = (((1,), (1,)), ((), ()))


def halves(value):
    high = value.astype(jnp.bfloat16)
    low = (value - high.astype(jnp.float32)).astype(jnp.bfloat16)
    return high, low


def kernel(
    n_cells, n_coef,
    poles_hbm, parents_hbm, ops_hbm, l2l_hbm, target_hbm, leaf_hbm, basis_hbm,
    local_ref, pot_ref,
    ops_ref, l2l_ref, target_ref, leaf_ref, basis_ref,
    gathered, elders, window_ref, hot_ref, leaf_hot_ref, pieces, out_buf, in_buf, total, partials,
    load_sem, g_send, g_recv, e_send, e_recv, w_send, w_recv, p_send, p_recv,
):
    row = lax.axis_index("cells")
    col = lax.axis_index("coef")
    noff, share, width = ops_ref.shape
    cd = target_ref.shape[1]
    tiles = leaf_ref.shape[0]
    lanes = leaf_ref.shape[1]

    loads = [
        pltpu.make_async_copy(src, dst, load_sem.at[i])
        for i, (src, dst) in enumerate(
            ((target_hbm, target_ref), (ops_hbm, ops_ref), (l2l_hbm, l2l_ref),
             (leaf_hbm, leaf_ref), (basis_hbm, basis_ref),
             (poles_hbm, gathered.at[col]), (parents_hbm, elders.at[col]))
        )
    ]
    for load in loads:
        load.start()

    barrier = pltpu.get_barrier_semaphore()
    for d in range(1, n_coef):
        pl.semaphore_signal(
            barrier, inc=1, device_id=(row, lax.rem(col + d, n_coef)),
            device_id_type=pl.DeviceIdType.MESH,
        )
    for w in WINDOWS:
        @pl.when((row + w >= 0) & (row + w < n_cells))
        def _():
            pl.semaphore_signal(
                barrier, inc=1, device_id=(row + w, col), device_id_type=pl.DeviceIdType.MESH
            )
    peers = n_coef - 1
    for w in WINDOWS:
        peers = peers + ((row + w >= 0) & (row + w < n_cells)).astype(jnp.int32)
    pl.semaphore_wait(barrier, peers)

    def gather_copy(k, d, slot):
        src, dst, send, recv = (
            (poles_hbm, gathered, g_send, g_recv), (parents_hbm, elders, e_send, e_recv)
        )[k]
        return pltpu.make_async_remote_copy(
            src_ref=src, dst_ref=dst.at[slot],
            send_sem=send.at[d - 1], recv_sem=recv.at[slot],
            device_id=(row, lax.rem(col + d, n_coef)), device_id_type=pl.DeviceIdType.MESH,
        )

    for k in range(2):
        for d in range(1, n_coef):
            gather_copy(k, d, col).start()
    iota = lax.broadcasted_iota(jnp.int32, (cd, cd), 0).astype(jnp.float32).astype(jnp.bfloat16)
    one = jnp.ones((cd, cd), jnp.bfloat16)
    zero = jnp.zeros((cd, cd), jnp.bfloat16)

    def one_hot(line):
        wide = jnp.broadcast_to(line.astype(jnp.float32), (16, line.shape[1])).astype(jnp.bfloat16)
        tall = jnp.concatenate([wide] * (cd // 16), axis=0)
        return jnp.where(tall == iota, one, zero)

    def span(first, count):
        return pl.ds(pl.multiple_of(first * cd, cd), count * cd)

    loads[0].wait()
    targets = target_ref[...] - row * cd
    window = targets // cd
    window_ref[...] = jnp.where(target_ref[...] >= 0, window, 8 * REACH).astype(jnp.float32)
    target_ref[...] = targets - window * cd

    def fill(first, count):
        hot_ref[:, span(first, count)] = jnp.concatenate(
            [one_hot(target_ref[pl.ds(first + j, 1), :]) for j in range(count)], axis=1
        )

    full = noff // GROUP
    lax.fori_loop(0, full, lambda i, _: fill(i * GROUP, GROUP), None)
    if noff % GROUP:
        fill(full * GROUP, noff % GROUP)

    loads[3].wait()
    leaf_hot_ref[...] = jnp.concatenate(
        [one_hot(leaf_ref[t : t + 1, :] - row * cd) for t in range(tiles)], axis=1
    )

    loads[5].wait()
    for d in range(1, n_coef):
        gather_copy(0, d, lax.rem(col + d, n_coef)).wait_recv()
    loads[1].wait()

    poles = jnp.concatenate([gathered[j] for j in range(n_coef)], axis=0)
    def far(first, count):
        block = ops_ref[pl.ds(first, count)].reshape(count * share, width)
        terms = jnp.dot(block, poles, preferred_element_type=jnp.float32)
        high, low = halves(terms)
        both = [
            jnp.concatenate([part[j * share : (j + 1) * share] for part in (high, low)], axis=0)
            for j in range(count)
        ]
        pieces[:, span(first, count)] = jnp.concatenate(both, axis=1)
        masked = [[] for _ in WINDOWS]
        for j in range(count):
            line = window_ref[pl.ds(first + j, 1), :]
            wide = jnp.broadcast_to(line, (16, cd)).astype(jnp.bfloat16)
            for i, w in enumerate(WINDOWS):
                keep = jnp.where(wide == w, one[:16], zero[:16])
                tall = jnp.concatenate([keep] * (2 * share // 16), axis=0)
                masked[i].append(both[j] * tall)
        stacked = jnp.concatenate([jnp.concatenate(m, axis=1) for m in masked], axis=0)
        return lax.dot_general(
            stacked, hot_ref[:, span(first, count)], NT, preferred_element_type=jnp.float32
        )

    def near(first, count):
        kept = []
        for j in range(count):
            line = window_ref[pl.ds(first + j, 1), :]
            wide = jnp.broadcast_to(line, (16, cd)).astype(jnp.bfloat16)
            keep = jnp.where(wide == 0, one[:16], zero[:16])
            tall = jnp.concatenate([keep] * (2 * share // 16), axis=0)
            kept.append(pieces[:, span(first + j, 1)] * tall)
        return lax.dot_general(
            jnp.concatenate(kept, axis=1), hot_ref[:, span(first, count)], NT,
            preferred_element_type=jnp.float32,
        )

    def over_offsets(step, rows):
        acc = jnp.zeros((rows, cd), jnp.float32)
        acc = lax.fori_loop(0, full, lambda i, a: a + step(i * GROUP, GROUP), acc)
        if noff % GROUP:
            acc = acc + step(full * GROUP, noff % GROUP)
        return acc

    def window_copy(i, w):
        return pltpu.make_async_remote_copy(
            src_ref=out_buf.at[i], dst_ref=in_buf.at[i],
            send_sem=w_send.at[i], recv_sem=w_recv.at[i],
            device_id=(row + w, col), device_id_type=pl.DeviceIdType.MESH,
        )

    sums = over_offsets(far, len(WINDOWS) * 2 * share)
    for i, w in enumerate(WINDOWS):
        base = 2 * share * i
        out_buf[i] = sums[base : base + share] + sums[base + share : base + 2 * share]
    for i, w in enumerate(WINDOWS):
        @pl.when((row + w >= 0) & (row + w < n_cells))
        def _():
            window_copy(i, w).start()

    sums = over_offsets(near, 2 * share)
    total[...] = sums[:share] + sums[share:]

    loads[2].wait()
    loads[6].wait()
    for d in range(1, n_coef):
        gather_copy(1, d, lax.rem(col + d, n_coef)).wait_recv()
    held = (elders.shape[1], cd)
    child = lax.broadcasted_iota(jnp.int32, held, 1)
    family = child // 8 == lax.broadcasted_iota(jnp.int32, held, 0)
    family = family.astype(jnp.float32).astype(jnp.bfloat16)
    wide_parents = jnp.concatenate(
        [
            lax.dot_general(
                elders[j], family, (((0,), (0,)), ((), ())), preferred_element_type=jnp.float32
            )
            for j in range(n_coef)
        ],
        axis=0,
    )
    octant = lax.broadcasted_iota(jnp.int32, wide_parents.shape, 1) % 8
    spread = jnp.concatenate(
        [jnp.where(octant == j, wide_parents, 0.0).astype(jnp.bfloat16) for j in range(8)], axis=0
    )
    shifts = jnp.concatenate([l2l_ref[j] for j in range(8)], axis=1)
    total[...] += jnp.dot(shifts, spread, preferred_element_type=jnp.float32)

    loads[4].wait()

    for i, w in enumerate(WINDOWS):
        @pl.when((row - w >= 0) & (row - w < n_cells))
        def _():
            window_copy(i, w).wait_recv()
            total[...] += in_buf[i]

    local = total[...]
    local_ref[...] = local
    columns = jnp.dot(
        jnp.concatenate(halves(local), axis=0), leaf_hot_ref[...], preferred_element_type=jnp.float32
    )
    columns = columns[:share] + columns[share:]
    partial = jnp.sum(columns * basis_ref[...].astype(jnp.float32), axis=0, keepdims=True)
    partials[col] = jnp.concatenate(
        [partial[:, t * lanes : (t + 1) * lanes] for t in range(tiles)], axis=0
    )

    def partial_copy(d, slot):
        return pltpu.make_async_remote_copy(
            src_ref=partials.at[slot], dst_ref=partials.at[slot],
            send_sem=p_send.at[d - 1], recv_sem=p_recv.at[slot],
            device_id=(row, lax.rem(col + d, n_coef)), device_id_type=pl.DeviceIdType.MESH,
        )

    for d in range(1, n_coef):
        partial_copy(d, col).start()
    for d in range(1, n_coef):
        partial_copy(d, lax.rem(col + d, n_coef)).wait_recv()
    potential = partials[0]
    for j in range(1, n_coef):
        potential = potential + partials[j]
    pot_ref[...] = potential

    for d in range(1, n_coef):
        gather_copy(0, d, col).wait_send()
        gather_copy(1, d, col).wait_send()
        partial_copy(d, col).wait_send()
    for i, w in enumerate(WINDOWS):
        @pl.when((row + w >= 0) & (row + w < n_cells))
        def _():
            window_copy(i, w).wait_send()


def on_device(
    n_cells, n_coef,
    multipole, parent_local, m2l_ops, l2l_ops, target_cell, particle_leaf, particle_basis,
):
    share, cd = multipole.shape
    noff = m2l_ops.shape[0]
    width = m2l_ops.shape[2]
    particles = particle_leaf.shape[0]
    lanes = 128
    tiles = particles // lanes
    leaf = particle_leaf.reshape(tiles, lanes)
    nwin = len(WINDOWS)
    dma = pltpu.SemaphoreType.DMA
    vmem = pl.BlockSpec(memory_space=pltpu.VMEM)
    hbm = pl.BlockSpec(memory_space=pltpu.HBM)
    local, potential = pl.pallas_call(
        functools.partial(kernel, n_cells, n_coef),
        out_shape=(
            jax.ShapeDtypeStruct((share, cd), jnp.float32),
            jax.ShapeDtypeStruct((tiles, lanes), jnp.float32),
        ),
        in_specs=[hbm] * 7,
        out_specs=(vmem, vmem),
        scratch_shapes=[
            pltpu.VMEM(m2l_ops.shape, m2l_ops.dtype),
            pltpu.VMEM(l2l_ops.shape, l2l_ops.dtype),
            pltpu.VMEM(target_cell.shape, target_cell.dtype),
            pltpu.VMEM(leaf.shape, leaf.dtype),
            pltpu.VMEM(particle_basis.shape, particle_basis.dtype),
            pltpu.VMEM((n_coef, share, cd), jnp.bfloat16),
            pltpu.VMEM((n_coef,) + parent_local.shape[::-1], jnp.bfloat16),
            pltpu.VMEM(target_cell.shape, jnp.float32),
            pltpu.VMEM((cd, noff * cd), jnp.bfloat16),
            pltpu.VMEM((cd, particles), jnp.bfloat16),
            pltpu.VMEM((2 * share, noff * cd), jnp.bfloat16),
            pltpu.VMEM((nwin, share, cd), jnp.float32),
            pltpu.VMEM((nwin, share, cd), jnp.float32),
            pltpu.VMEM((share, cd), jnp.float32),
            pltpu.VMEM((n_coef, tiles, lanes), jnp.float32),
            dma((7,)),
            dma((n_coef - 1,)),
            dma((n_coef,)),
            dma((n_coef - 1,)),
            dma((n_coef,)),
            dma((nwin,)),
            dma((nwin,)),
            dma((n_coef - 1,)),
            dma((n_coef,)),
        ],
        compiler_params=pltpu.CompilerParams(
            collective_id=0, has_side_effects=True, vmem_limit_bytes=67043328
        ),
    )(multipole, parent_local.T, m2l_ops, l2l_ops, target_cell, leaf, particle_basis)
    return local, potential.reshape(particles)


def solution(mesh):
    return jax.shard_map(
        functools.partial(on_device, mesh.shape["cells"], mesh.shape["coef"]),
        mesh=mesh,
        in_specs=(
            P("coef", "cells"),
            P("coef", "cells"),
            P(None, "coef", None),
            P(None, "coef", None),
            P(None, "cells"),
            P("cells"),
            P("coef", "cells"),
        ),
        out_specs=(P("coef", "cells"), P("cells")),
        check_vma=False,
    )
```

profile of v0, /device:TPU:0, one launch (start us, length us, event | category | flops | bytes accessed | tf_op | source)
XLA Modules:
  0.0 23.8 jit_solution(12119011058331626364)
XLA Ops:
  0.6 20.6 %shard_map.86 = (f32[32,128]{1,0:T(8,128)}, f32[16,128]{1,0:T(8,128)}) custom-call(bf16[32,128]{1,0:T(8,128)(2,1)} %poles_hbm.1, bf16[16,32]{1,0:T(8,128)(2,1)} %bitcast.5, bf16[189,32,128]{2,1,0:T(8,128)(2,1)} %ops_hbm.1, bf16[8,32,128]{2,1,0:T(8,128)(2,1)} %l2l_hbm.1, s32[189,128]{1,0:T(8,128)} %target_hbm.1, s32[16,128]{1,0:T(8,128)} %bitcast.3, ...), custom_call_target="tpu_custom_call" | custom-call | tf_op jit(solution)/shard_map/pallas_call | solution.py:262
  21.2 1.3 %copy.11 = f32[32,128]{1,0:T(8,128)} copy(f32[32,128]{1,0:T(8,128)} %get-tuple-element.8) | data formatting | bytes 32768
  22.5 1.3 %copy.12 = f32[2048]{0:T(1024)} copy(f32[2048]{0:T(1024)} %bitcast.4) | data formatting | bytes 16384
where the time goes:
time: 24.2 us; the launch traced here: 23.8 us
  Pallas kernels  20.6 us (85%)
  local copies, waits for them, and re-layouts  2.62 us (11%)
  between operations  0.64 us (3%)
    pallas_call x1, Pallas kernels, on_device(): pl.pallas_call(functools.partial(kernel, n_cells, n_coef), out_shape=(jax...  20.6 us
    unnamed x2, local copies, waits for them, and re-layouts  2.62 us

commit v1 on v0

v1 whole, which is shorter than its diff:
```python
import functools

import jax
import jax.numpy as jnp
from jax import lax
from jax.experimental import pallas as pl
from jax.experimental.pallas import tpu as pltpu
from jax.sharding import PartitionSpec as P

WINDOWS = (-2, 2, -1, 1)
NT = (((1,), (1,)), ((), ()))
TN = (((0,), (0,)), ((), ()))
BF = jnp.bfloat16
HOT = jnp.float8_e4m3fn
MESH = pl.DeviceIdType.MESH


def halves(value):
    high = value.astype(BF)
    low = (value - high.astype(jnp.float32)).astype(BF)
    return high, low


def kernel(
    n_cells, n_coef, group,
    poles_hbm, parents_hbm, ops_hbm, l2l_hbm, target_hbm, leaf_hbm, basis_hbm,
    local_ref, pot_ref,
    ops_ref, l2l_ref, target_ref, leaf_ref, basis_ref,
    gathered, elders, hot_far, hot_near, leaf_hot, outer_ref, rows_ref,
    out_buf, in_buf, partials,
    load_sem, g_send, g_recv, e_send, e_recv, w_send, w_recv, p_send, p_recv,
):
    row = lax.axis_index("cells")
    col = lax.axis_index("coef")
    noff, share, width = ops_ref.shape
    cd = target_ref.shape[1]
    tiles, lanes = leaf_ref.shape

    loads = [
        pltpu.make_async_copy(src, dst, load_sem.at[i])
        for i, (src, dst) in enumerate(
            ((target_hbm, target_ref), (ops_hbm, ops_ref), (l2l_hbm, l2l_ref),
             (leaf_hbm, leaf_ref), (basis_hbm, basis_ref),
             (poles_hbm, gathered.at[col]), (parents_hbm, elders.at[col]))
        )
    ]
    for load in loads:
        load.start()

    barrier = pltpu.get_barrier_semaphore()
    for d in range(1, n_coef):
        pl.semaphore_signal(
            barrier, inc=1, device_id=(row, lax.rem(col + d, n_coef)), device_id_type=MESH
        )
    for w in WINDOWS:
        @pl.when((row + w >= 0) & (row + w < n_cells))
        def _():
            pl.semaphore_signal(barrier, inc=1, device_id=(row + w, col), device_id_type=MESH)
    peers = n_coef - 1
    for w in WINDOWS:
        peers = peers + ((row + w >= 0) & (row + w < n_cells)).astype(jnp.int32)
    pl.semaphore_wait(barrier, peers)

    def gather_copy(k, d, slot):
        src, dst, send, recv = (
            (poles_hbm, gathered, g_send, g_recv), (parents_hbm, elders, e_send, e_recv)
        )[k]
        return pltpu.make_async_remote_copy(
            src_ref=src, dst_ref=dst.at[slot],
            send_sem=send.at[d - 1], recv_sem=recv.at[slot],
            device_id=(row, lax.rem(col + d, n_coef)), device_id_type=MESH,
        )

    for k in range(2):
        for d in range(1, n_coef):
            gather_copy(k, d, col).start()

    def one_hot(line, count):
        wide = jnp.broadcast_to(line, (16, line.shape[1])).astype(BF)
        tall = jnp.concatenate([wide] * (count // 16), axis=0)
        iota = lax.broadcasted_iota(jnp.int32, tall.shape, 0).astype(jnp.float32).astype(BF)
        return jnp.where(tall == iota, jnp.ones_like(tall), jnp.zeros_like(tall)).astype(HOT)

    def span(first):
        return pl.ds(pl.multiple_of(first * cd, cd), cd)

    def fill_far(g):
        first = g * group
        target = target_ref[pl.ds(first, group), :]
        t = target - row * cd
        outer = (t < -cd) | (t >= 2 * cd)
        slot = jnp.where(t < 0, t + jnp.where(outer, 2 * cd, cd), t - jnp.where(outer, cd, 0))
        far = (target >= 0) & ((t < 0) | (t >= cd))
        slot = jnp.where(far, slot, -1).astype(jnp.float32)
        swap = ((t < -cd) | ((t >= cd) & (t < 2 * cd))).astype(jnp.float32)
        for j in range(group):
            hot_far[:, span(first + j)] = one_hot(slot[j : j + 1], 2 * cd)
            outer_ref[:, span(first + j)] = jnp.broadcast_to(
                swap[j : j + 1], (16, cd)
            ).astype(BF)

    def fill_near(g):
        first = g * group
        target = target_ref[pl.ds(first, group), :]
        t = target - row * cd
        slot = jnp.where((target >= 0) & (t >= 0) & (t < cd), t, -1).astype(jnp.float32)
        for j in range(group):
            hot_near[:, span(first + j)] = one_hot(slot[j : j + 1], cd)

    loads[0].wait()
    lax.fori_loop(0, noff // group, lambda g, _: fill_far(g), None)

    loads[5].wait()
    for d in range(1, n_coef):
        gather_copy(0, d, lax.rem(col + d, n_coef)).wait_recv()
    loads[1].wait()

    poles = jnp.concatenate([gathered[j] for j in range(n_coef)], axis=0)
    high, low = halves(
        jnp.dot(ops_ref[...].reshape(noff * share, width), poles,
                preferred_element_type=jnp.float32)
    )
    for j in range(noff):
        both = jnp.concatenate(
            [part[j * share : (j + 1) * share] for part in (high, low)], axis=0
        )
        rows_ref[: 2 * share, j * cd : (j + 1) * cd] = both
        keep = jnp.concatenate([outer_ref[:, j * cd : (j + 1) * cd]] * (2 * share // 16), axis=0)
        rows_ref[2 * share :, j * cd : (j + 1) * cd] = both * keep

    def window_copy(i, w):
        return pltpu.make_async_remote_copy(
            src_ref=out_buf.at[i], dst_ref=in_buf.at[i],
            send_sem=w_send.at[i], recv_sem=w_recv.at[i],
            device_id=(row + w, col), device_id_type=MESH,
        )

    sums = lax.dot_general(rows_ref[...], hot_far[...], NT, preferred_element_type=jnp.float32)
    every = sums[:share] + sums[share : 2 * share]
    some = sums[2 * share : 3 * share] + sums[3 * share :]
    rest = every - some
    for i, part in enumerate((some[:, :cd], rest[:, cd:], rest[:, :cd], some[:, cd:])):
        out_buf[i] = part
    for i, w in enumerate(WINDOWS):
        @pl.when((row + w >= 0) & (row + w < n_cells))
        def _():
            window_copy(i, w).start()

    lax.fori_loop(0, noff // group, lambda g, _: fill_near(g), None)
    sums = lax.dot_general(
        rows_ref[: 2 * share, :], hot_near[...], NT, preferred_element_type=jnp.float32
    )
    total = sums[:share] + sums[share:]

    loads[2].wait()
    loads[6].wait()
    for d in range(1, n_coef):
        gather_copy(1, d, lax.rem(col + d, n_coef)).wait_recv()
    held = (elders.shape[1], cd)
    child = lax.broadcasted_iota(jnp.int32, held, 1)
    family = child // 8 == lax.broadcasted_iota(jnp.int32, held, 0)
    family = family.astype(jnp.float32).astype(BF)
    wide_parents = jnp.concatenate(
        [
            lax.dot_general(elders[j], family, TN, preferred_element_type=jnp.float32)
            for j in range(n_coef)
        ],
        axis=0,
    )
    octant = lax.broadcasted_iota(jnp.int32, wide_parents.shape, 1) % 8
    spread = jnp.concatenate(
        [jnp.where(octant == j, wide_parents, 0.0).astype(BF) for j in range(8)], axis=0
    )
    shifts = jnp.concatenate([l2l_ref[j] for j in range(8)], axis=1)
    total = total + jnp.dot(shifts, spread, preferred_element_type=jnp.float32)
    local_ref[...] = total

    loads[3].wait()
    for t in range(tiles):
        leaf = (leaf_ref[t : t + 1, :] - row * cd).astype(jnp.float32)
        leaf_hot[:, t * lanes : (t + 1) * lanes] = one_hot(leaf, cd)
    loads[4].wait()

    for i, w in enumerate(WINDOWS):
        @pl.when((row - w >= 0) & (row - w < n_cells))
        def _():
            window_copy(i, w).wait_recv()
            local_ref[...] += in_buf[i]

    columns = jnp.dot(
        jnp.concatenate(halves(local_ref[...]), axis=0), leaf_hot[...],
        preferred_element_type=jnp.float32,
    )
    columns = columns[:share] + columns[share:]
    partial = jnp.sum(columns * basis_ref[...].astype(jnp.float32), axis=0, keepdims=True)
    partials[col] = jnp.concatenate(
        [partial[:, t * lanes : (t + 1) * lanes] for t in range(tiles)], axis=0
    )

    def partial_copy(d, slot):
        return pltpu.make_async_remote_copy(
            src_ref=partials.at[slot], dst_ref=partials.at[slot],
            send_sem=p_send.at[d - 1], recv_sem=p_recv.at[slot],
            device_id=(row, lax.rem(col + d, n_coef)), device_id_type=MESH,
        )

    for d in range(1, n_coef):
        partial_copy(d, col).start()
    for d in range(1, n_coef):
        partial_copy(d, lax.rem(col + d, n_coef)).wait_recv()
    potential = partials[0]
    for j in range(1, n_coef):
        potential = potential + partials[j]
    pot_ref[...] = potential

    for d in range(1, n_coef):
        gather_copy(0, d, col).wait_send()
        gather_copy(1, d, col).wait_send()
        partial_copy(d, col).wait_send()
    for i, w in enumerate(WINDOWS):
        @pl.when((row + w >= 0) & (row + w < n_cells))
        def _():
            window_copy(i, w).wait_send()


def on_device(
    n_cells, n_coef,
    multipole, parent_local, m2l_ops, l2l_ops, target_cell, particle_leaf, particle_basis,
):
    share, cd = multipole.shape
    noff = m2l_ops.shape[0]
    particles = particle_leaf.shape[0]
    lanes = 128
    tiles = particles // lanes
    group = max(g for g in range(1, 33) if noff % g == 0)
    leaf = particle_leaf.reshape(tiles, lanes)
    nwin = len(WINDOWS)
    dma = pltpu.SemaphoreType.DMA
    vmem = pl.BlockSpec(memory_space=pltpu.VMEM)
    hbm = pl.BlockSpec(memory_space=pltpu.HBM)
    local, potential = pl.pallas_call(
        functools.partial(kernel, n_cells, n_coef, group),
        out_shape=(pltpu.VMEM((share, cd), jnp.float32), pltpu.VMEM((tiles, lanes), jnp.float32)),
        in_specs=[hbm] * 7,
        out_specs=(vmem, vmem),
        scratch_shapes=[
            pltpu.VMEM(m2l_ops.shape, m2l_ops.dtype),
            pltpu.VMEM(l2l_ops.shape, l2l_ops.dtype),
            pltpu.VMEM(target_cell.shape, target_cell.dtype),
            pltpu.VMEM(leaf.shape, leaf.dtype),
            pltpu.VMEM(particle_basis.shape, particle_basis.dtype),
            pltpu.VMEM((n_coef, share, cd), BF),
            pltpu.VMEM((n_coef,) + parent_local.shape[::-1], BF),
            pltpu.VMEM((2 * cd, noff * cd), HOT),
            pltpu.VMEM((cd, noff * cd), HOT),
            pltpu.VMEM((cd, particles), HOT),
            pltpu.VMEM((16, noff * cd), BF),
            pltpu.VMEM((4 * share, noff * cd), BF),
            pltpu.VMEM((nwin, share, cd), jnp.float32),
            pltpu.VMEM((nwin, share, cd), jnp.float32),
            pltpu.VMEM((n_coef, tiles, lanes), jnp.float32),
            dma((7,)),
            dma((n_coef - 1,)),
            dma((n_coef,)),
            dma((n_coef - 1,)),
            dma((n_coef,)),
            dma((nwin,)),
            dma((nwin,)),
            dma((n_coef - 1,)),
            dma((n_coef,)),
        ],
        compiler_params=pltpu.CompilerParams(
            collective_id=0, has_side_effects=True, vmem_limit_bytes=60000000
        ),
    )(multipole, parent_local.T, m2l_ops, l2l_ops, target_cell, leaf, particle_basis)
    return local, potential.reshape(particles)


def solution(mesh):
    return jax.shard_map(
        functools.partial(on_device, mesh.shape["cells"], mesh.shape["coef"]),
        mesh=mesh,
        in_specs=(
            P("coef", "cells"),
            P("coef", "cells"),
            P(None, "coef", None),
            P(None, "coef", None),
            P(None, "cells"),
            P("cells"),
            P("coef", "cells"),
        ),
        out_specs=(P("coef", "cells"), P("cells")),
        check_vma=False,
    )
```

time: 24.2 us -> 18.1 us (0.75)
  Pallas kernels: 20.6 us -> 16.1 us
  local copies, waits for them, and re-layouts: 2.62 us -> 1.21 us
    pallas_call x1, Pallas kernels: 20.6 us -> 16.1 us  [on_device(): pl.pallas_call(functools.partial(kernel, n_cells, n_coef, group), out_sha...]
    unnamed x2, local copies, waits for them, and re-layouts: 2.62 us -> 1.21 us
where the time goes in v1:
time: 18.1 us; the launch traced here: 17.9 us
  Pallas kernels  16.1 us (89%)
  local copies, waits for them, and re-layouts  1.21 us (7%)
  between operations  0.64 us (4%)
    pallas_call x1, Pallas kernels, on_device(): pl.pallas_call(functools.partial(kernel, n_cells, n_coef, group), out_sha...  16.1 us
    unnamed x2, local copies, waits for them, and re-layouts  1.21 us

profile of v1, /device:TPU:0, one launch (start us, length us, event | category | flops | bytes accessed | tf_op | source)
XLA Modules:
  0.0 17.9 jit_solution(4425418603036307315)
XLA Ops:
  0.6 16.1 %shard_map.86 = (f32[32,128]{1,0:T(8,128)S(1)}, f32[16,128]{1,0:T(8,128)S(1)}) custom-call(bf16[32,128]{1,0:T(8,128)(2,1)} %poles_hbm.1, bf16[16,32]{1,0:T(8,128)(2,1)} %bitcast.5, bf16[189,32,128]{2,1,0:T(8,128)(2,1)} %ops_hbm.1, bf16[8,32,128]{2,1,0:T(8,128)(2,1)} %l2l_hbm.1, s32[189,128]{1,0:T(8,128)} %target_hbm.1, s32[16,128]{1,0:T(8,128)} %bitcast.4, ...), custom_call_target="tpu_custom_call" | custom-call | tf_op jit(solution)/shard_map/pallas_call | solution.py:241
  16.7 0.6 %copy.11 = f32[32,128]{1,0:T(8,128)} copy(f32[32,128]{1,0:T(8,128)S(1)} %get-tuple-element.6) | data formatting | bytes 32768
  17.3 0.6 %copy.12 = f32[2048]{0:T(1024)} copy(f32[2048]{0:T(1024)S(1)} %bitcast.3) | data formatting | bytes 16384

commit v2 on v1

--- a/solution.py
+++ b/solution.py
@@ -7,7 +7,7 @@
 from jax.experimental.pallas import tpu as pltpu
 from jax.sharding import PartitionSpec as P
 
-WINDOWS = (-2, 2, -1, 1)
+WINDOWS = (-1, 1, -2, 2)
 NT = (((1,), (1,)), ((), ()))
 TN = (((0,), (0,)), ((), ()))
 BF = jnp.bfloat16
@@ -39,9 +39,9 @@
     loads = [
         pltpu.make_async_copy(src, dst, load_sem.at[i])
         for i, (src, dst) in enumerate(
-            ((target_hbm, target_ref), (ops_hbm, ops_ref), (l2l_hbm, l2l_ref),
-             (leaf_hbm, leaf_ref), (basis_hbm, basis_ref),
-             (poles_hbm, gathered.at[col]), (parents_hbm, elders.at[col]))
+            ((poles_hbm, gathered.at[col]), (parents_hbm, elders.at[col]),
+             (target_hbm, target_ref), (leaf_hbm, leaf_ref), (ops_hbm, ops_ref),
+             (l2l_hbm, l2l_ref), (basis_hbm, basis_ref))
         )
     ]
     for load in loads:
@@ -60,10 +60,13 @@
     for w in WINDOWS:
         peers = peers + ((row + w >= 0) & (row + w < n_cells)).astype(jnp.int32)
     pl.semaphore_wait(barrier, peers)
+    loads[0].wait()
+    loads[1].wait()
 
     def gather_copy(k, d, slot):
         src, dst, send, recv = (
-            (poles_hbm, gathered, g_send, g_recv), (parents_hbm, elders, e_send, e_recv)
+            (gathered.at[col], gathered, g_send, g_recv),
+            (elders.at[col], elders, e_send, e_recv),
         )[k]
         return pltpu.make_async_remote_copy(
             src_ref=src, dst_ref=dst.at[slot],
@@ -75,14 +78,18 @@
         for d in range(1, n_coef):
             gather_copy(k, d, col).start()
 
-    def one_hot(line, count):
+    def one_hot(line, count, value=1.0):
         wide = jnp.broadcast_to(line, (16, line.shape[1])).astype(BF)
         tall = jnp.concatenate([wide] * (count // 16), axis=0)
         iota = lax.broadcasted_iota(jnp.int32, tall.shape, 0).astype(jnp.float32).astype(BF)
-        return jnp.where(tall == iota, jnp.ones_like(tall), jnp.zeros_like(tall)).astype(HOT)
-
-    def span(first):
-        return pl.ds(pl.multiple_of(first * cd, cd), cd)
+        hit = jnp.full(tall.shape, value, jnp.float32).astype(BF)
+        return jnp.where(tall == iota, hit, jnp.zeros_like(tall)).astype(HOT)
+
+    half = 2 * pl.cdiv(noff, 4)
+
+    def sign(j):
+        return jnp.where(j < half, 1.0, -1.0)
+
 
     def fill_far(g):
         first = g * group
@@ -94,8 +101,10 @@
         slot = jnp.where(far, slot, -1).astype(jnp.float32)
         swap = ((t < -cd) | ((t >= cd) & (t < 2 * cd))).astype(jnp.float32)
         for j in range(group):
-            hot_far[:, span(first + j)] = one_hot(slot[j : j + 1], 2 * cd)
-            outer_ref[:, span(first + j)] = jnp.broadcast_to(
+            hot_far[first + j] = one_hot(
+                slot[j : j + 1], 2 * cd, sign(first + j)
+            )
+            outer_ref[first + j] = jnp.broadcast_to(
                 swap[j : j + 1], (16, cd)
             ).astype(BF)
 
@@ -105,15 +114,19 @@
         t = target - row * cd
         slot = jnp.where((target >= 0) & (t >= 0) & (t < cd), t, -1).astype(jnp.float32)
         for j in range(group):
-            hot_near[:, span(first + j)] = one_hot(slot[j : j + 1], cd)
-
-    loads[0].wait()
+            hot_near[first + j] = one_hot(slot[j : j + 1], cd, sign(first + j))
+
+    loads[2].wait()
     lax.fori_loop(0, noff // group, lambda g, _: fill_far(g), None)
-
-    loads[5].wait()
+    lax.fori_loop(0, noff // group, lambda g, _: fill_near(g), None)
+    loads[3].wait()
+    for t in range(tiles):
+        leaf = (leaf_ref[t : t + 1, :] - row * cd).astype(jnp.float32)
+        leaf_hot[:, t * lanes : (t + 1) * lanes] = one_hot(leaf, cd)
+
     for d in range(1, n_coef):
         gather_copy(0, d, lax.rem(col + d, n_coef)).wait_recv()
-    loads[1].wait()
+    loads[4].wait()
 
     poles = jnp.concatenate([gathered[j] for j in range(n_coef)], axis=0)
     high, low = halves(
@@ -124,9 +137,8 @@
         both = jnp.concatenate(
             [part[j * share : (j + 1) * share] for part in (high, low)], axis=0
         )
-        rows_ref[: 2 * share, j * cd : (j + 1) * cd] = both
-        keep = jnp.concatenate([outer_ref[:, j * cd : (j + 1) * cd]] * (2 * share // 16), axis=0)
-        rows_ref[2 * share :, j * cd : (j + 1) * cd] = both * keep
+        keep = jnp.concatenate([outer_ref[j]] * (2 * share // 16), axis=0)
+        rows_ref[j] = jnp.concatenate([both, both * keep], axis=0)
 
     def window_copy(i, w):
         return pltpu.make_async_remote_copy(
@@ -135,27 +147,37 @@
             device_id=(row + w, col), device_id_type=MESH,
         )
 
-    sums = lax.dot_general(rows_ref[...], hot_far[...], NT, preferred_element_type=jnp.float32)
+    def beside(ref, count, first, last):
+        return jnp.concatenate([ref[j, :count] for j in range(first, last)], axis=1)
+
+    def scatter(hot, count):
+        plus, minus = (
+            lax.dot_general(
+                beside(rows_ref, count, *part), beside(hot, hot.shape[1], *part), NT,
+                preferred_element_type=jnp.float32,
+            )
+            for part in ((0, half), (half, noff))
+        )
+        return plus - minus
+
+    sums = scatter(hot_far, 4 * share)
     every = sums[:share] + sums[share : 2 * share]
     some = sums[2 * share : 3 * share] + sums[3 * share :]
     rest = every - some
-    for i, part in enumerate((some[:, :cd], rest[:, cd:], rest[:, :cd], some[:, cd:])):
+    for i, part in enumerate((rest[:, :cd], some[:, cd:], some[:, :cd], rest[:, cd:])):
         out_buf[i] = part
     for i, w in enumerate(WINDOWS):
         @pl.when((row + w >= 0) & (row + w < n_cells))
         def _():
             window_copy(i, w).start()
 
-    lax.fori_loop(0, noff // group, lambda g, _: fill_near(g), None)
-    sums = lax.dot_general(
-        rows_ref[: 2 * share, :], hot_near[...], NT, preferred_element_type=jnp.float32
-    )
+    loads[5].wait()
+    loads[6].wait()
+    for d in range(1, n_coef):
+        gather_copy(1, d, lax.rem(col + d, n_coef)).wait_recv()
+    sums = scatter(hot_near, 2 * share)
     total = sums[:share] + sums[share:]
 
-    loads[2].wait()
-    loads[6].wait()
-    for d in range(1, n_coef):
-        gather_copy(1, d, lax.rem(col + d, n_coef)).wait_recv()
     held = (elders.shape[1], cd)
     child = lax.broadcasted_iota(jnp.int32, held, 1)
     family = child // 8 == lax.broadcasted_iota(jnp.int32, held, 0)
@@ -174,12 +196,6 @@
     shifts = jnp.concatenate([l2l_ref[j] for j in range(8)], axis=1)
     total = total + jnp.dot(shifts, spread, preferred_element_type=jnp.float32)
     local_ref[...] = total
-
-    loads[3].wait()
-    for t in range(tiles):
-        leaf = (leaf_ref[t : t + 1, :] - row * cd).astype(jnp.float32)
-        leaf_hot[:, t * lanes : (t + 1) * lanes] = one_hot(leaf, cd)
-    loads[4].wait()
 
     for i, w in enumerate(WINDOWS):
         @pl.when((row - w >= 0) & (row - w < n_cells))
@@ -251,11 +267,11 @@
             pltpu.VMEM(particle_basis.shape, particle_basis.dtype),
             pltpu.VMEM((n_coef, share, cd), BF),
             pltpu.VMEM((n_coef,) + parent_local.shape[::-1], BF),
-            pltpu.VMEM((2 * cd, noff * cd), HOT),
-            pltpu.VMEM((cd, noff * cd), HOT),
+            pltpu.VMEM((noff, 2 * cd, cd), HOT),
+            pltpu.VMEM((noff, cd, cd), HOT),
             pltpu.VMEM((cd, particles), HOT),
-            pltpu.VMEM((16, noff * cd), BF),
-            pltpu.VMEM((4 * share, noff * cd), BF),
+            pltpu.VMEM((noff, 16, cd), BF),
+            pltpu.VMEM((noff, 4 * share, cd), BF),
             pltpu.VMEM((nwin, share, cd), jnp.float32),
             pltpu.VMEM((nwin, share, cd), jnp.float32),
             pltpu.VMEM((n_coef, tiles, lanes), jnp.float32),

time: 18.1 us -> 16.9 us (0.934)
  Pallas kernels: 16.1 us -> 14.9 us
    pallas_call x1, Pallas kernels: 16.1 us -> 14.9 us  [on_device(): pl.pallas_call(functools.partial(kernel, n_cells, n_coef, group), out_sha...]
where the time goes in v2:
time: 16.9 us; the launch traced here: 16.7 us
  Pallas kernels  14.9 us (88%)
  local copies, waits for them, and re-layouts  1.21 us (7%)
  between operations  0.64 us (4%)
    pallas_call x1, Pallas kernels, on_device(): pl.pallas_call(functools.partial(kernel, n_cells, n_coef, group), out_sha...  14.9 us
    unnamed x2, local copies, waits for them, and re-layouts  1.21 us

profile of v2, /device:TPU:0, one launch (start us, length us, event | category | flops | bytes accessed | tf_op | source)
XLA Modules:
  0.0 16.7 jit_solution(1007373787892656231)
XLA Ops:
  0.6 14.9 %shard_map.86 = (f32[32,128]{1,0:T(8,128)S(1)}, f32[16,128]{1,0:T(8,128)S(1)}) custom-call(bf16[32,128]{1,0:T(8,128)(2,1)} %poles_hbm.1, bf16[16,32]{1,0:T(8,128)(2,1)} %bitcast.5, bf16[189,32,128]{2,1,0:T(8,128)(2,1)} %ops_hbm.1, bf16[8,32,128]{2,1,0:T(8,128)(2,1)} %l2l_hbm.1, s32[189,128]{1,0:T(8,128)} %target_hbm.1, s32[16,128]{1,0:T(8,128)} %bitcast.4, ...), custom_call_target="tpu_custom_call" | custom-call | tf_op jit(solution)/shard_map/pallas_call | solution.py:257
  15.5 0.6 %copy.11 = f32[32,128]{1,0:T(8,128)} copy(f32[32,128]{1,0:T(8,128)S(1)} %get-tuple-element.6) | data formatting | bytes 32768
  16.1 0.6 %copy.12 = f32[2048]{0:T(1024)} copy(f32[2048]{0:T(1024)S(1)} %bitcast.3) | data formatting | bytes 16384

commit v3 on v2

--- a/solution.py
+++ b/solution.py
@@ -7,7 +7,7 @@
 from jax.experimental.pallas import tpu as pltpu
 from jax.sharding import PartitionSpec as P
 
-WINDOWS = (-1, 1, -2, 2)
+WINDOWS = (-2, 2, -1, 1)
 NT = (((1,), (1,)), ((), ()))
 TN = (((0,), (0,)), ((), ()))
 BF = jnp.bfloat16
@@ -164,7 +164,7 @@
     every = sums[:share] + sums[share : 2 * share]
     some = sums[2 * share : 3 * share] + sums[3 * share :]
     rest = every - some
-    for i, part in enumerate((rest[:, :cd], some[:, cd:], some[:, :cd], rest[:, cd:])):
+    for i, part in enumerate((some[:, :cd], rest[:, cd:], rest[:, :cd], some[:, cd:])):
         out_buf[i] = part
     for i, w in enumerate(WINDOWS):
         @pl.when((row + w >= 0) & (row + w < n_cells))
@@ -289,6 +289,26 @@
             collective_id=0, has_side_effects=True, vmem_limit_bytes=60000000
         ),
     )(multipole, parent_local.T, m2l_ops, l2l_ops, target_cell, leaf, particle_basis)
+    def put(a, b, c, d, sem):
+        one = pltpu.make_async_copy(a, c, sem.at[0])
+        two = pltpu.make_async_copy(b, d, sem.at[1])
+        one.start()
+        two.start()
+        one.wait()
+        two.wait()
+
+    local = pltpu.with_memory_space_constraint(local, pltpu.VMEM)
+    potential = pltpu.with_memory_space_constraint(potential, pltpu.VMEM)
+    local, potential = pl.pallas_call(
+        put,
+        out_shape=(
+            jax.ShapeDtypeStruct(local.shape, local.dtype),
+            jax.ShapeDtypeStruct(potential.shape, potential.dtype),
+        ),
+        in_specs=[vmem, vmem],
+        out_specs=(hbm, hbm),
+        scratch_shapes=[dma((2,))],
+    )(local, potential)
     return local, potential.reshape(particles)
 
 

time: 16.9 us -> 16.1 us (0.953)
  local copies, waits for them, and re-layouts: 1.21 us -> 0 us
  Pallas kernels: 14.9 us -> 15.3 us
    unnamed x2 -> x0, local copies, waits for them, and re-layouts: 1.21 us -> none
    pallas_call x0 -> x1, Pallas kernels: none -> 0.63 us  [on_device(): pl.pallas_call(put, out_shape=(jax.ShapeDtypeStruct(local.shape, local.dt...]
    pallas_call x1, Pallas kernels: 14.9 us -> 14.7 us  [on_device(): pl.pallas_call(functools.partial(kernel, n_cells, n_coef, group), out_sha...]
where the time goes in v3:
time: 16.1 us; the launch traced here: 16 us
  Pallas kernels  15.3 us (95%)
  between operations  0.64 us (4%)
    pallas_call x1, Pallas kernels, on_device(): pl.pallas_call(functools.partial(kernel, n_cells, n_coef, group), out_sha...  14.7 us
    pallas_call x1, Pallas kernels, on_device(): pl.pallas_call(put, out_shape=(jax.ShapeDtypeStruct(local.shape, local.dt...  0.63 us

profile of v3, /device:TPU:0, one launch (start us, length us, event | category | flops | bytes accessed | tf_op | source)
XLA Modules:
  0.0 16.0 jit_solution(10426778186594928407)
XLA Ops:
  0.6 14.7 %shard_map.86 = (f32[32,128]{1,0:T(8,128)S(1)}, f32[16,128]{1,0:T(8,128)S(1)}) custom-call(bf16[32,128]{1,0:T(8,128)(2,1)} %poles_hbm.1, bf16[16,32]{1,0:T(8,128)(2,1)} %bitcast.4, bf16[189,32,128]{2,1,0:T(8,128)(2,1)} %ops_hbm.1, bf16[8,32,128]{2,1,0:T(8,128)(2,1)} %l2l_hbm.1, s32[189,128]{1,0:T(8,128)} %target_hbm.1, s32[16,128]{1,0:T(8,128)} %bitcast.3, ...), custom_call_target="tpu_custom_call" | custom-call | tf_op jit(solution)/shard_map/pallas_call | solution.py:257
  15.3 0.6 %shard_map.87 = (f32[32,128]{1,0:T(8,128)}, f32[16,128]{1,0:T(8,128)}) custom-call(f32[32,128]{1,0:T(8,128)S(1)} %get-tuple-element.6.a, f32[16,128]{1,0:T(8,128)S(1)} %get-tuple-element.7.b), custom_call_target="tpu_custom_call" | custom-call | tf_op jit(solution)/shard_map/pallas_call | solution.py:302

commit v4 on v3

--- a/solution.py
+++ b/solution.py
@@ -36,6 +36,15 @@
     cd = target_ref.shape[1]
     tiles, lanes = leaf_ref.shape
 
+    barrier = pltpu.get_barrier_semaphore()
+    for d in range(1, n_coef):
+        pl.semaphore_signal(
+            barrier, inc=1, device_id=(row, lax.rem(col + d, n_coef)), device_id_type=MESH
+        )
+    for w in WINDOWS:
+        @pl.when((row + w >= 0) & (row + w < n_cells))
+        def _():
+            pl.semaphore_signal(barrier, inc=1, device_id=(row + w, col), device_id_type=MESH)
     loads = [
         pltpu.make_async_copy(src, dst, load_sem.at[i])
         for i, (src, dst) in enumerate(
@@ -47,15 +56,6 @@
     for load in loads:
         load.start()
 
-    barrier = pltpu.get_barrier_semaphore()
-    for d in range(1, n_coef):
-        pl.semaphore_signal(
-            barrier, inc=1, device_id=(row, lax.rem(col + d, n_coef)), device_id_type=MESH
-        )
-    for w in WINDOWS:
-        @pl.when((row + w >= 0) & (row + w < n_cells))
-        def _():
-            pl.semaphore_signal(barrier, inc=1, device_id=(row + w, col), device_id_type=MESH)
     peers = n_coef - 1
     for w in WINDOWS:
         peers = peers + ((row + w >= 0) & (row + w < n_cells)).astype(jnp.int32)
@@ -129,16 +129,20 @@
     loads[4].wait()
 
     poles = jnp.concatenate([gathered[j] for j in range(n_coef)], axis=0)
-    high, low = halves(
-        jnp.dot(ops_ref[...].reshape(noff * share, width), poles,
-                preferred_element_type=jnp.float32)
-    )
-    for j in range(noff):
-        both = jnp.concatenate(
-            [part[j * share : (j + 1) * share] for part in (high, low)], axis=0
-        )
-        keep = jnp.concatenate([outer_ref[j]] * (2 * share // 16), axis=0)
-        rows_ref[j] = jnp.concatenate([both, both * keep], axis=0)
+    def terms(first, last):
+        high, low = halves(
+            jnp.dot(ops_ref[first:last].reshape((last - first) * share, width), poles,
+                    preferred_element_type=jnp.float32)
+        )
+        for j in range(first, last):
+            here = slice((j - first) * share, (j - first + 1) * share)
+            both = jnp.concatenate([high[here], low[here]], axis=0)
+            keep = jnp.concatenate([outer_ref[j]] * (2 * share // 16), axis=0)
+            rows_ref[j] = jnp.concatenate([both, both * keep], axis=0)
+
+    cuts = (0, half, noff)
+    for first, last in zip(cuts, cuts[1:]):
+        terms(first, last)
 
     def window_copy(i, w):
         return pltpu.make_async_remote_copy(

time: 16.1 us -> 16 us (level)
  no operation moved by 1% of the time
where the time goes in v4:
time: 16 us; the launch traced here: 15.9 us
  Pallas kernels  15.2 us (95%)
  between operations  0.64 us (4%)
    pallas_call x1, Pallas kernels, on_device(): pl.pallas_call(functools.partial(kernel, n_cells, n_coef, group), out_sha...  14.6 us
    pallas_call x1, Pallas kernels, on_device(): pl.pallas_call(put, out_shape=(jax.ShapeDtypeStruct(local.shape, local.dt...  0.63 us

profile of v4, /device:TPU:0, one launch (start us, length us, event | category | flops | bytes accessed | tf_op | source)
XLA Modules:
  0.0 15.9 jit_solution(14785797113298163661)
XLA Ops:
  0.6 14.6 %shard_map.86 = (f32[32,128]{1,0:T(8,128)S(1)}, f32[16,128]{1,0:T(8,128)S(1)}) custom-call(bf16[32,128]{1,0:T(8,128)(2,1)} %poles_hbm.1, bf16[16,32]{1,0:T(8,128)(2,1)} %bitcast.4, bf16[189,32,128]{2,1,0:T(8,128)(2,1)} %ops_hbm.1, bf16[8,32,128]{2,1,0:T(8,128)(2,1)} %l2l_hbm.1, s32[189,128]{1,0:T(8,128)} %target_hbm.1, s32[16,128]{1,0:T(8,128)} %bitcast.3, ...), custom_call_target="tpu_custom_call" | custom-call | tf_op jit(solution)/shard_map/pallas_call | solution.py:261
  15.2 0.6 %shard_map.87 = (f32[32,128]{1,0:T(8,128)}, f32[16,128]{1,0:T(8,128)}) custom-call(f32[32,128]{1,0:T(8,128)S(1)} %get-tuple-element.6.a, f32[16,128]{1,0:T(8,128)S(1)} %get-tuple-element.7.b), custom_call_target="tpu_custom_call" | custom-call | tf_op jit(solution)/shard_map/pallas_call | solution.py:306

commit v5 on v4

--- a/solution.py
+++ b/solution.py
@@ -207,15 +207,18 @@
             window_copy(i, w).wait_recv()
             local_ref[...] += in_buf[i]
 
-    columns = jnp.dot(
-        jnp.concatenate(halves(local_ref[...]), axis=0), leaf_hot[...],
-        preferred_element_type=jnp.float32,
-    )
-    columns = columns[:share] + columns[share:]
-    partial = jnp.sum(columns * basis_ref[...].astype(jnp.float32), axis=0, keepdims=True)
-    partials[col] = jnp.concatenate(
-        [partial[:, t * lanes : (t + 1) * lanes] for t in range(tiles)], axis=0
-    )
+    rows = jnp.concatenate(halves(local_ref[...]), axis=0)
+    middle = pl.cdiv(tiles, 2)
+    for first, last in ((0, middle), (middle, tiles)):
+        reach = slice(first * lanes, last * lanes)
+        columns = jnp.dot(rows, leaf_hot[:, reach], preferred_element_type=jnp.float32)
+        columns = columns[:share] + columns[share:]
+        partial = jnp.sum(
+            columns * basis_ref[:, reach].astype(jnp.float32), axis=0, keepdims=True
+        )
+        partials[col, first:last] = jnp.concatenate(
+            [partial[:, t * lanes : (t + 1) * lanes] for t in range(last - first)], axis=0
+        )
 
     def partial_copy(d, slot):
         return pltpu.make_async_remote_copy(

time: 16 us -> 16 us (level)
  no operation moved by 1% of the time
where the time goes in v5:
time: 16 us; the launch traced here: 15.9 us
  Pallas kernels  15.2 us (95%)
  between operations  0.64 us (4%)
    pallas_call x1, Pallas kernels, on_device(): pl.pallas_call(functools.partial(kernel, n_cells, n_coef, group), out_sha...  14.6 us
    pallas_call x1, Pallas kernels, on_device(): pl.pallas_call(put, out_shape=(jax.ShapeDtypeStruct(local.shape, local.dt...  0.63 us

profile of v5, /device:TPU:0, one launch (start us, length us, event | category | flops | bytes accessed | tf_op | source)
XLA Modules:
  0.0 15.9 jit_solution(14785797113298163661)
XLA Ops:
  0.6 14.6 %shard_map.86 = (f32[32,128]{1,0:T(8,128)S(1)}, f32[16,128]{1,0:T(8,128)S(1)}) custom-call(bf16[32,128]{1,0:T(8,128)(2,1)} %poles_hbm.1, bf16[16,32]{1,0:T(8,128)(2,1)} %bitcast.4, bf16[189,32,128]{2,1,0:T(8,128)(2,1)} %ops_hbm.1, bf16[8,32,128]{2,1,0:T(8,128)(2,1)} %l2l_hbm.1, s32[189,128]{1,0:T(8,128)} %target_hbm.1, s32[16,128]{1,0:T(8,128)} %bitcast.3, ...), custom_call_target="tpu_custom_call" | custom-call | tf_op jit(solution)/shard_map/pallas_call | solution.py:264
  15.2 0.6 %shard_map.87 = (f32[32,128]{1,0:T(8,128)}, f32[16,128]{1,0:T(8,128)}) custom-call(f32[32,128]{1,0:T(8,128)S(1)} %get-tuple-element.6.a, f32[16,128]{1,0:T(8,128)S(1)} %get-tuple-element.7.b), custom_call_target="tpu_custom_call" | custom-call | tf_op jit(solution)/shard_map/pallas_call | solution.py:309
